TPU v7x, 32 devices: a whole 2x2x4 slice. The times are simulated.
32 devices in a mesh: dom: 32 (over z, y, x, core).
Axes of the slice: x: 2, y: 2, z: 4, core: 2. Of those that a mesh axis runs over, the one named last changes fastest.
Arguments:
- right_side: float32 [32768, 3], P('dom'), may hold values from -10 to 10
- fine_diagonal: float32 [32768, 3], P('dom'), may hold values from 2 to 4
- fine_columns: int32 [32768, 27], P('dom'), may hold values from 0 to 32767, as said below
- fine_blocks: float32 [32768, 27, 3, 3], P('dom'), may hold values from -0.625 to 0.625
- aggregate_of_node: int32 [32768], P('dom'), may hold values from 0 to 31, as said below
- coarse_row_of_aggregate: int32 [1024], P('dom'), may hold values from 0 to 1023, as said below
- coarse_diagonal: float32 [1024, 3], P('dom'), may hold values from 2 to 4
- coarse_columns: int32 [1024, 27], P('dom'), may hold values from 0 to 1023
- coarse_blocks: float32 [1024, 27, 3, 3], P('dom'), may hold values from -0.625 to 0.625
Outputs:
- solution: float32 [32768, 3], P('dom')
- correction: float32 [1024, 3], P('dom')
Inputs may be any that keep to these rules, and one draw needn't show every extreme that they name: Every entry of fine_columns differs from its row number by at most 256, and some entry by exactly 256. `aggregate_of_node`: on each device every aggregate number 0 to 31 is used by at least one of its nodes. coarse_row_of_aggregate is a permutation of 0 to 1023; among the 32 aggregates of one device (an aligned block of entries) at most 8 get rows of any one owner, and exactly 8 for some owner.
All inputs are finite; a program needn't handle non-finite values.
Results may differ from a plain program's by a relative error of at most 0.0003.
Values sent between devices are 32-bit elements.
A program may use at most 64 MiB of HBM per device.

v0:
```python
import jax
import jax.numpy as jnp
from jax import lax
from jax.sharding import PartitionSpec as P

CAP = 8
WIN = 256
SWEEPS = 2
CSWEEPS = 6


damping = 0.7
highest = lax.Precision.HIGHEST


def padded_2(value, sides, width, wrap):
    for axis, dim in sides:
        peers, length = lax.axis_size(axis), value.shape[dim]
        up = [(i, (i + 1) % peers) for i in range(peers if wrap else peers - 1)]
        down = [(j, i) for i, j in up]
        last = lax.slice_in_dim(value, length - width, length, axis=dim)
        initial = lax.slice_in_dim(value, 0, width, axis=dim)
        before = lax.ppermute(last, axis, up)
        after = lax.ppermute(initial, axis, down)
        value = jnp.concatenate([before, value, after], axis=dim)
    return value


def couple(blocks, nearby):
    return jnp.sum(blocks * nearby[:, :, None, :], axis=(1, 3))


def apply_fine(field, fine_diagonal, fine_columns, fine_blocks):
    row_count = fine_columns.shape[0]
    padded = padded_2(field, (("dom", 0),), WIN, False)
    first_row = lax.axis_index("dom") * row_count - WIN
    local_columns = (fine_columns - first_row).astype(jnp.int32)
    nearby = padded[local_columns]
    return fine_diagonal * field - couple(fine_blocks, nearby)


def apply_coarse(field, coarse_diagonal, coarse_columns, coarse_blocks):
    gathered = lax.all_gather(field, "dom", axis=0, tiled=True)
    nearby = gathered[coarse_columns]
    return coarse_diagonal * field - couple(coarse_blocks, nearby)


def per_device(
    right_side,
    fine_diagonal,
    fine_columns,
    fine_blocks,
    aggregate_of_node,
    coarse_row_of_aggregate,
    coarse_diagonal,
    coarse_columns,
    coarse_blocks,
):
    solution = damping * right_side / fine_diagonal
    for sweep in range(SWEEPS - 1):
        solution = (
            solution
            + damping
            * (right_side - apply_fine(solution, fine_diagonal, fine_columns, fine_blocks))
            / fine_diagonal
        )
    residual = right_side - apply_fine(solution, fine_diagonal, fine_columns, fine_blocks)
    aggregate_count = coarse_diagonal.shape[0]
    devices = lax.axis_size("dom")
    aggregate_ids = jnp.arange(aggregate_count, dtype=jnp.int32)
    sums_here = jax.ops.segment_sum(residual, aggregate_of_node, num_segments=aggregate_count)
    owners = coarse_row_of_aggregate // aggregate_count
    member = (owners[:, None] == jnp.arange(devices, dtype=jnp.int32)[None, :]).astype(jnp.float32)
    earlier = (aggregate_ids[None, :] < aggregate_ids[:, None]).astype(jnp.float32)
    before = jnp.dot(earlier, member, precision=highest)
    position = jnp.sum(before * member, axis=1).astype(jnp.int32)
    bucket = (owners * CAP + position).astype(jnp.int32)
    local_rows = (coarse_row_of_aggregate - owners * aggregate_count).astype(jnp.int32)
    slot_out = jnp.full((devices * CAP,), aggregate_count, jnp.int32).at[bucket].set(local_rows)
    slot_in = lax.all_to_all(slot_out, "dom", split_axis=0, concat_axis=0, tiled=True)
    outgoing = jnp.zeros((devices * CAP, 3), jnp.float32).at[bucket].set(sums_here)
    arrived = lax.all_to_all(outgoing, "dom", split_axis=0, concat_axis=0, tiled=True)
    coarse_rhs = jnp.zeros((aggregate_count, 3), jnp.float32).at[slot_in].add(arrived, mode="drop")
    correction = damping * coarse_rhs / coarse_diagonal
    for sweep in range(CSWEEPS - 1):
        correction = (
            correction
            + damping
            * (
                coarse_rhs
                - apply_coarse(correction, coarse_diagonal, coarse_columns, coarse_blocks)
            )
            / coarse_diagonal
        )
    sending = jnp.take(correction, slot_in, axis=0, mode="fill", fill_value=0.0)
    returned = lax.all_to_all(sending, "dom", split_axis=0, concat_axis=0, tiled=True)
    label_values = returned[bucket]
    solution = solution + label_values[aggregate_of_node]
    for sweep in range(SWEEPS):
        solution = (
            solution
            + damping
            * (right_side - apply_fine(solution, fine_diagonal, fine_columns, fine_blocks))
            / fine_diagonal
        )
    return (solution, correction)


def solution(mesh):
    return jax.shard_map(
        per_device,
        mesh=mesh,
        in_specs=(
            P("dom", None),
            P("dom", None),
            P("dom", None),
            P("dom", None, None, None),
            P("dom"),
            P("dom"),
            P("dom", None),
            P("dom", None),
            P("dom", None, None, None),
        ),
        out_specs=(P("dom", None), P("dom", None)),
        check_vma=False,
    )
```

profile of v0, /device:TPU:7, one launch (start us, length us, event | category | flops | bytes accessed | tf_op | source)
XLA Modules:
  0.0 707.4 jit_solution(2365184784400468609)
XLA Ops:
  0.6 0.8 multiply_divide_fusion
  1.4 3.7 collective-permute-start
  5.1 1.9 collective-permute-start.1
  7.0 0.7 multiply_subtract_fusion
  7.9 0.7 scatter_custom_fusion
  8.5 0.7 all_to_all.24
  9.2 6.3 all-to-all-start
  15.6 0.9 compare_select_fusion
  16.7 0.4 reshape.62
  17.3 3.2 all-to-all-done
  20.4 0.5 broadcast.165
  21.0 0.7 reduce.3
  21.8 0.3 copy.475
  22.1 91.4 %gather_fusion = f32[27648,3]{1,0:T(8,128)} fusion(f32[1536,3]{1,0:T(8,128)S(1)} %copy.475, s32[27648]{0:T(1024)S(1)} %broadcast_clamp_fusion), kind=kCustom, calls=%fused_computation | custom fusion | bytes 774144 | tf_op jit(solution)/shard_map/gather | solution.py:38
  113.5 8.3 %copy.476 = f32[27648,3]{0,1:T(4,128)S(1)} copy(f32[27648,3]{1,0:T(8,128)} %gather_fusion) | data formatting | bytes 663552 | tf_op jit(solution)/shard_map/gather | solution.py:38
  121.7 3.0 reshape.61
  124.7 1.9 copy.477
  126.9 4.5 collective-permute-start.2
  131.4 1.9 collective-permute-start.3
  133.4 4.8 collective-permute-done.3
  138.1 0.3 copy.479
  138.4 91.4 %gather_fusion.1 = f32[27648,3]{1,0:T(8,128)} fusion(f32[1536,3]{1,0:T(8,128)S(1)} %copy.479, s32[27648]{0:T(1024)S(1)} %broadcast_clamp_fusion), kind=kCustom, calls=%fused_computation.1 | custom fusion | bytes 774144 | tf_op jit(solution)/shard_map/gather | solution.py:38
  229.8 8.3 %copy.480 = f32[27648,3]{0,1:T(4,128)S(1)} copy(f32[27648,3]{1,0:T(8,128)} %gather_fusion.1) | data formatting | bytes 663552 | tf_op jit(solution)/shard_map/gather | solution.py:38
  238.1 3.0 reshape.69
  241.1 1.9 copy.481
  243.4 6.0 scatter_custom_fusion.1
  249.4 0.7 scatter_custom_fusion.2
  250.1 0.9 copy.484
  251.0 2.8 all-to-all-start.1
  253.8 5.3 all-to-all-done.1
  259.4 1.4 scatter_custom_fusion.3
  260.9 35.4 %all-gather = f32[32,32,3]{1,2,0:T(4,128)S(1)} all-gather(f32[1,32,3]{1,2,0:T(4,128)S(1)} %fusion.12), channel_id=1, replica_groups=mesh['dom'=32] {'dom'}, dimensions={0}, use_global_device_ids=true | all-gather | bytes 12672 | tf_op jit(solution)/shard_map/all_gather | solution.py:43
  296.6 1.9 gather_fusion.2
  299.0 37.5 %all-gather.1 = f32[32,32,3]{1,2,0:T(4,128)S(1)} all-gather(f32[1,32,3]{1,2,0:T(4,128)S(1)} %bitcast.51), channel_id=1, replica_groups=mesh['dom'=32] {'dom'}, dimensions={0}, use_global_device_ids=true | all-gather | bytes 12672 | tf_op jit(solution)/shard_map/all_gather | solution.py:43
  336.7 1.9 gather_fusion.3
  339.0 37.7 %all-gather.2 = f32[32,32,3]{1,2,0:T(4,128)S(1)} all-gather(f32[1,32,3]{1,2,0:T(4,128)S(1)} %bitcast.49), channel_id=1, replica_groups=mesh['dom'=32] {'dom'}, dimensions={0}, use_global_device_ids=true | all-gather | bytes 12672 | tf_op jit(solution)/shard_map/all_gather | solution.py:43
  377.0 1.9 gather_fusion.4
  379.3 37.5 %all-gather.3 = f32[32,32,3]{1,2,0:T(4,128)S(1)} all-gather(f32[1,32,3]{1,2,0:T(4,128)S(1)} %bitcast.50), channel_id=1, replica_groups=mesh['dom'=32] {'dom'}, dimensions={0}, use_global_device_ids=true | all-gather | bytes 12672 | tf_op jit(solution)/shard_map/all_gather | solution.py:43
  417.0 1.9 gather_fusion.5
  419.3 37.5 %all-gather.4 = f32[32,32,3]{1,2,0:T(4,128)S(1)} all-gather(f32[1,32,3]{1,2,0:T(4,128)S(1)} %bitcast.48), channel_id=1, replica_groups=mesh['dom'=32] {'dom'}, dimensions={0}, use_global_device_ids=true | all-gather | bytes 12672 | tf_op jit(solution)/shard_map/all_gather | solution.py:43
  457.1 1.9 gather_fusion.6
  459.5 0.7 gather_fusion.7
  460.5 0.7 broadcast_select_fusion
  461.2 6.6 all-to-all-start.2
  467.7 5.4 all-to-all-done.2
  473.4 0.6 gather_fusion.8
  474.0 2.8 gather_fusion.9
  477.0 4.3 collective-permute-start.4
  481.3 1.9 collective-permute-start.5
  483.3 4.8 collective-permute-done.5
  488.1 0.3 copy.507
  488.4 91.4 %gather_fusion.10 = f32[27648,3]{1,0:T(8,128)} fusion(f32[1536,3]{1,0:T(8,128)S(1)} %copy.507, s32[27648]{0:T(1024)S(1)} %broadcast_clamp_fusion), kind=kCustom, calls=%fused_computation.10 | custom fusion | bytes 774144 | tf_op jit(solution)/shard_map/gather | solution.py:38
  579.7 8.3 %copy.508 = f32[27648,3]{0,1:T(4,128)S(1)} copy(f32[27648,3]{1,0:T(8,128)} %gather_fusion.10) | data formatting | bytes 663552 | tf_op jit(solution)/shard_map/gather | solution.py:38
  588.0 3.0 reshape.141
  591.0 1.9 copy.509
  593.1 1.9 collective-permute-start.6
  595.0 2.4 collective-permute-start.7
  597.4 4.3 collective-permute-done.7
  601.8 0.3 copy.510
  602.1 91.4 %gather_fusion.11 = f32[27648,3]{1,0:T(8,128)} fusion(f32[1536,3]{1,0:T(8,128)S(1)} %copy.510, s32[27648]{0:T(1024)S(1)} %broadcast_clamp_fusion), kind=kCustom, calls=%fused_computation.11 | custom fusion | bytes 774144 | tf_op jit(solution)/shard_map/gather | solution.py:38
  693.4 8.3 %copy.511 = f32[27648,3]{0,1:T(4,128)S(1)} copy(f32[27648,3]{1,0:T(8,128)} %gather_fusion.11) | data formatting | bytes 663552 | tf_op jit(solution)/shard_map/gather | solution.py:38
  701.7 3.0 reshape.149
  704.7 1.9 copy.512
  706.8 0.6 divide_add_fusion
  (83 shorter events, 6.2 us)
Async XLA Ops:
  0.6 16.5 %copy-start.5 = (s32[32,27]{1,0:T(8,128)S(1)}, s32[32,27]{1,0:T(8,128)}, u32[]{:S(2)}) copy-start(s32[32,27]{1,0:T(8,128)} %param.16) | copy-start | bytes 10372
  0.6 16.6 %copy-start.7 = (s32[1024]{0:T(1024)S(1)}, s32[1024]{0:T(1024)}, u32[]{:S(2)}) copy-start(s32[1024]{0:T(1024)} %param.13) | copy-start | bytes 12292
  1.4 20.3 %collective-permute-start = (f32[256,3]{0,1:T(4,128)S(1)}, f32[256,3]{0,1:T(4,128)S(1)}, u32[]{:S(2)}, u32[]{:S(2)}) collective-permute-start(f32[256,3]{0,1:T(4,128)S(1)} %get-tuple-element.22), channel_id=1, source_target_pairs={{0,1},{1,2},{2,3},{3,4},{4,5},{5,6},{6,7},{7,8},{8,9},{9,10},{10,1... | collective-permute-start | bytes 9224 | tf_op jit(solution)/shard_map/ppermute | solution.py:23
  5.1 16.6 %collective-permute-start.1 = (f32[256,3]{0,1:T(4,128)S(1)}, f32[256,3]{0,1:T(4,128)S(1)}, u32[]{:S(2)}, u32[]{:S(2)}) collective-permute-start(f32[256,3]{0,1:T(4,128)S(1)} %get-tuple-element.23), channel_id=1, source_target_pairs={{1,0},{2,1},{3,2},{4,3},{5,4},{6,5},{7,6},{8,7},{9,8},{10,9},{11,1... | collective-permute-start | bytes 9224 | tf_op jit(solution)/shard_map/ppermute | solution.py:24
  9.2 11.2 %all-to-all-start = ((s32[32,8,1]{1,2,0:T(1,128)}), s32[32,8,1]{1,2,0:T(1,128)S(1)}, u32[]{:S(2)}, u32[]{:S(2)}) async-start(s32[32,8,1]{1,2,0:T(1,128)} %bitcast), calls=%async_computation | async-start | bytes 32768 | tf_op jit(solution)/shard_map/all_to_all | solution.py:80
  121.7 4.9 copy-start
  124.7 2.1 copy-start.2
  124.7 2.1 copy-start.3
  126.9 6.5 collective-permute-start.2
  131.4 6.7 collective-permute-start.3
  243.0 17.9 %copy-start.4 = (f32[32,3]{0,1:T(4,128)S(1)}, f32[32,3]{0,1:T(4,128)}, u32[]{:S(2)}) copy-start(f32[32,3]{0,1:T(4,128)} %param.15) | copy-start | bytes 1156
  251.0 8.1 %all-to-all-start.1 = ((f32[32,8,3]{1,2,0:T(4,128)}), f32[32,8,3]{1,2,0:T(4,128)S(1)}, u32[]{:S(2)}, u32[]{:S(2)}) async-start(f32[32,8,3]{1,2,0:T(4,128)} %copy.484), calls=%async_computation.1 | async-start | bytes 131072 | tf_op jit(solution)/shard_map/all_to_all | solution.py:82
  296.6 2.2 copy-start.1
  459.4 17.4 %copy-start.6 = (f32[32,3]{0,1:T(4,128)}, f32[32,3]{0,1:T(4,128)S(1)}, u32[]{:S(2)}) copy-start(f32[32,3]{0,1:T(4,128)S(1)} %divide_add_fusion.3) | copy-start | bytes 1156
  461.2 12.0 %all-to-all-start.2 = ((f32[32,8,3]{1,2,0:T(4,128)}), f32[32,8,3]{1,2,0:T(4,128)S(1)}, u32[]{:S(2)}, u32[]{:S(2)}) async-start(f32[32,8,3]{1,2,0:T(4,128)} %broadcast_select_fusion), calls=%async_computation.2 | async-start | bytes 131072 | tf_op jit(solution)/shard_map/all_to_all | solution.py:96
  477.0 6.2 collective-permute-start.4
  481.3 6.7 collective-permute-start.5
  593.1 4.3 collective-permute-start.6
  595.0 6.7 collective-permute-start.7
where the time goes:
time: 708 us; the launch traced here: 707 us
  local copies, waits for them, and re-layouts  441 us (62%)
  blocking collectives  186 us (26%)
  starting transfers between devices  38.3 us (5%)
  waiting for transfers between devices  27.8 us (4%)
  other arithmetic  13.2 us (2%)
    gather x16, local copies, waits for them, and re-layouts, apply_fine(): nearby = padded[local_columns]  418 us
    all_gather x5, blocking collectives, apply_coarse(): gathered = lax.all_gather(field, 'dom', axis=0, tiled=True)  186 us
    ppermute x4, starting transfers between devices, padded_2(): before = lax.ppermute(last, axis, up)  14.5 us
  transfers between devices with their start and end apart: 11, of which 6 were waited for; matrix products, arithmetic and copies ran while one was open for 1% of the time, Pallas kernels for 0%

commit v1 on v0

v1 whole, which is shorter than its diff:
```python
import functools

import jax
import jax.numpy as jnp
from jax import lax
from jax.experimental import pallas as pl
from jax.experimental.pallas import tpu as pltpu
from jax.sharding import PartitionSpec as P

WIN = 256
SWEEPS = 2
CSWEEPS = 6
LANES = 128

damping = 0.7


def pick(source, lane):
    return jnp.take_along_axis(source, lane, axis=1, mode="promise_in_bounds")


def fine_kernel(smooth, pad_ref, index_ref, block_ref, diagonal_ref, right_ref, out_ref):
    slots, chunks, _ = index_ref.shape
    margin = WIN // LANES
    sources = [[pad_ref[c, j : j + chunks, :] for j in range(2 * margin + 1)] for c in range(3)]
    total = [jnp.zeros((chunks, LANES), jnp.float32) for _ in range(3)]
    for k in range(slots):
        position = index_ref[k]
        lane, chunk = position & (LANES - 1), position >> 7
        masks = [chunk == j for j in range(2 * margin + 1)]
        for c in range(3):
            near = pick(sources[c][0], lane)
            for j in range(1, 2 * margin + 1):
                near = jnp.where(masks[j], pick(sources[c][j], lane), near)
            for i in range(3):
                total[i] = total[i] + block_ref[k, i, c] * near
    for i in range(3):
        field = pad_ref[i, margin : margin + chunks, :]
        residual = right_ref[i] - (diagonal_ref[i] * field - total[i])
        if smooth:
            out_ref[i] = field + damping * residual / diagonal_ref[i]
        else:
            out_ref[i] = residual


def far_pick(values, position):
    lane, chunk = position & (LANES - 1), position >> 7
    out = []
    for value in values:
        count = value.shape[0]
        near = jnp.zeros(position.shape, jnp.float32)
        for j in range(count):
            row = jnp.broadcast_to(value[j : j + 1, :], position.shape)
            near = jnp.where(chunk == j, pick(row, lane), near)
        out.append(near)
    return out


def coarse_kernel(sums_ref, inverse_ref, column_ref, block_ref, diagonal_ref, label_ref, own_ref, field_ref,
                  out_ref, correction_ref, rhs_ref, next_ref):
    slots, chunks, _ = column_ref.shape
    group = 8
    groups = chunks // group
    for g in range(groups):
        rows = pl.ds(g * group, group)
        picked = far_pick([sums_ref[c] for c in range(3)], inverse_ref[rows, :])
        for c in range(3):
            rhs_ref[c, rows, :] = picked[c]
            correction_ref[c, rows, :] = damping * picked[c] / diagonal_ref[c, rows, :]

    def sweep(_, carry):
        for g in range(groups):
            rows = pl.ds(g * group, group)

            def slot(k, total):
                total = list(total)
                near = far_pick([correction_ref[c] for c in range(3)], column_ref[k, rows, :])
                for i in range(3):
                    for c in range(3):
                        total[i] = total[i] + block_ref[k, i, c, rows, :] * near[c]
                return tuple(total)

            zero = jnp.zeros((group, LANES), jnp.float32)
            total = lax.fori_loop(0, slots, slot, (zero,) * 3, unroll=9 if groups == 1 else 1)
            for i in range(3):
                diagonal, field = diagonal_ref[i, rows, :], correction_ref[i, rows, :]
                residual = rhs_ref[i, rows, :] - (diagonal * field - total[i])
                next_ref[i, rows, :] = field + damping * residual / diagonal
        correction_ref[...] = next_ref[...]
        return carry

    lax.fori_loop(0, CSWEEPS - 1, sweep, 0)
    label = label_ref[...]
    row = pick(jnp.broadcast_to(own_ref[...], label.shape), label)
    picked = far_pick([correction_ref[c] for c in range(3)], row)
    for c in range(3):
        out_ref[c] = field_ref[c] + picked[c]


def per_device(
    right_side,
    fine_diagonal,
    fine_columns,
    fine_blocks,
    aggregate_of_node,
    coarse_row_of_aggregate,
    coarse_diagonal,
    coarse_columns,
    coarse_blocks,
):
    devices, me = lax.axis_size("dom"), lax.axis_index("dom")
    nodes, slots = fine_columns.shape
    chunks, margin = nodes // LANES, WIN // LANES
    own, coarse_slots = coarse_columns.shape
    rows = own * devices
    up = [(i, i + 1) for i in range(devices - 1)]
    down = [(j, i) for i, j in up]

    right = right_side.T.reshape(3, chunks, LANES)
    diagonal = fine_diagonal.T.reshape(3, chunks, LANES)
    blocks = jnp.transpose(fine_blocks, (1, 2, 3, 0)).reshape(slots, 3, 3, chunks, LANES)
    shift = LANES * jnp.arange(chunks, dtype=jnp.int32)[None, :, None]
    index = fine_columns.T.reshape(slots, chunks, LANES) - (me * nodes - WIN) - shift
    label = aggregate_of_node.reshape(chunks, LANES)

    floats = jnp.concatenate(
        [jnp.transpose(coarse_blocks, (1, 2, 3, 0)).reshape(coarse_slots * 9, own), coarse_diagonal.T], axis=0
    )
    integers = jnp.concatenate([coarse_columns.T, coarse_row_of_aggregate[None, :]], axis=0)
    floats = lax.all_gather(floats, "dom", axis=1, tiled=True)
    integers = lax.all_gather(integers, "dom", axis=1, tiled=True)
    grid = (rows // LANES, LANES)
    all_blocks = floats[: coarse_slots * 9].reshape((coarse_slots, 3, 3) + grid)
    all_diagonal = floats[coarse_slots * 9 :].reshape((3,) + grid)
    all_columns = integers[:coarse_slots].reshape((coarse_slots,) + grid)
    permutation = integers[coarse_slots]
    ids = jnp.arange(rows, dtype=jnp.int32)
    inverse = jnp.sum(jnp.where(permutation[:, None] == ids[None, :], ids[:, None], 0), axis=0).reshape(grid)
    own_rows = jnp.pad(coarse_row_of_aggregate, (0, LANES - own)).reshape(1, LANES)

    def fine(field, smooth):
        before = lax.ppermute(field[:, chunks - margin :], "dom", up)
        after = lax.ppermute(field[:, :margin], "dom", down)
        padded = jnp.concatenate([before, field, after], axis=1)
        return pl.pallas_call(
            functools.partial(fine_kernel, smooth),
            out_shape=jax.ShapeDtypeStruct((3, chunks, LANES), jnp.float32),
        )(padded, index, blocks, diagonal, right)

    field = damping * right / diagonal
    for _ in range(SWEEPS - 1):
        field = fine(field, True)
    residual = fine(field, False)
    member = aggregate_of_node[None, :] == jnp.arange(own, dtype=jnp.int32)[:, None]
    flat = residual.reshape(3, nodes)
    sums = jnp.sum(jnp.where(member[None], flat[:, None, :], 0.0), axis=2)
    sums = lax.all_gather(sums, "dom", axis=1, tiled=True).reshape((3,) + grid)
    field, correction = pl.pallas_call(
        coarse_kernel,
        out_shape=(
            jax.ShapeDtypeStruct((3, chunks, LANES), jnp.float32),
            jax.ShapeDtypeStruct((3,) + grid, jnp.float32),
        ),
        scratch_shapes=[pltpu.VMEM((3,) + grid, jnp.float32), pltpu.VMEM((3,) + grid, jnp.float32)],
    )(sums, inverse, all_columns, all_blocks, all_diagonal, label, own_rows, field)
    correction = lax.dynamic_slice_in_dim(correction.reshape(3, rows), me * own, own, axis=1).T
    for _ in range(SWEEPS):
        field = fine(field, True)
    return (field.reshape(3, nodes).T, correction)


def solution(mesh):
    return jax.shard_map(
        per_device,
        mesh=mesh,
        in_specs=(
            P("dom", None),
            P("dom", None),
            P("dom", None),
            P("dom", None, None, None),
            P("dom"),
            P("dom"),
            P("dom", None),
            P("dom", None),
            P("dom", None, None, None),
        ),
        out_specs=(P("dom", None), P("dom", None)),
        check_vma=False,
    )
```

time: 708 us -> 190 us (0.27)
  local copies, waits for them, and re-layouts: 441 us -> 15.9 us
  blocking collectives: 186 us -> 115 us
  waiting for transfers between devices: 27.8 us -> 8.08 us
  starting transfers between devices: 38.3 us -> 19.7 us
  Pallas kernels: 0 us -> 17.1 us
    gather x36 -> x0, local copies, waits for them, and re-layouts: 433 us -> none  [the longest x16 418 us: apply_fine(): nearby = padded[local_columns]]
    all_gather x5 -> x3, blocking collectives: 186 us -> 115 us  [the longest x1 43.3 us: per_device(): floats = lax.all_gather(floats, 'dom', axis=1, tiled=True)]
    pallas_call x0 -> x5, Pallas kernels: none -> 17.1 us  [the longest x4 9.99 us: fine(): pl.pallas_call(functools.partial(fine_kernel, smooth), out_shape=jax.Shap...]
    all_to_all x3 -> x0, starting transfers between devices: 15.7 us -> none  [the longest x1 6.57 us: per_device(): lax.all_to_all(sending, 'dom', split_axis=0, concat_axis=0, tiled=True)]
    all_to_all x3 -> x0, waiting for transfers between devices: 13.9 us -> none  [the longest x1 5.41 us: per_device(): lax.all_to_all(sending, 'dom', split_axis=0, concat_axis=0, tiled=True)]
    scatter-add x2 -> x0, other arithmetic: 7.44 us -> none  [the longest x1 6.01 us: per_device(): jax.ops.segment_sum(residual, aggregate_of_node, num_segments=aggregate_c...]
  transfers between devices with their start and end apart: 11 -> 8, of which waited for: 6 -> 3; matrix products, arithmetic and copies ran while one was open for 1% -> 8% of each run, Pallas kernels for 0% -> 0%
where the time goes in v1:
time: 190 us; the launch traced here: 186 us
  blocking collectives  115 us (61%)
  starting transfers between devices  19.7 us (10%)
  Pallas kernels  17.1 us (9%)
  local copies, waits for them, and re-layouts  15.9 us (8%)
  other arithmetic  8.92 us (5%)
  waiting for transfers between devices  8.08 us (4%)
    all_gather x1, blocking collectives, per_device(): floats = lax.all_gather(floats, 'dom', axis=1, tiled=True)  43.3 us
    all_gather x1, blocking collectives, per_device(): integers = lax.all_gather(integers, 'dom', axis=1, tiled=True)  36.3 us
    all_gather x1, blocking collectives, per_device(): sums = lax.all_gather(sums, 'dom', axis=1, tiled=True).reshape((3,) + grid)  35.7 us
    ppermute x4, starting transfers between devices, fine(): before = lax.ppermute(field[:, chunks - margin:], 'dom', up)  11.1 us
    pallas_call x4, Pallas kernels, fine(): pl.pallas_call(functools.partial(fine_kernel, smooth), out_shape=jax.Shap...  9.99 us
    ppermute x4, starting transfers between devices, fine(): after = lax.ppermute(field[:, :margin], 'dom', down)  8.62 us
    ppermute x4, waiting for transfers between devices, fine(): after = lax.ppermute(field[:, :margin], 'dom', down)  8.07 us
    pallas_call x1, Pallas kernels, per_device(): pl.pallas_call(coarse_kernel, out_shape=(jax.ShapeDtypeStruct((3, chunks,...  7.07 us
  transfers between devices with their start and end apart: 8, of which 3 were waited for; matrix products, arithmetic and copies ran while one was open for 8% of the time, Pallas kernels for 0%

profile of v1, /device:TPU:7, one launch (start us, length us, event | category | flops | bytes accessed | tf_op | source)
XLA Modules:
  0.0 185.9 jit_solution(7868820521638644339)
XLA Ops:
  0.6 0.0 copy-start.1
  0.6 1.3 multiply_divide_fusion
  2.0 3.7 %collective-permute-start = (f32[3,2,128]{2,1,0:T(2,128)S(1)}, f32[3,2,128]{2,1,0:T(2,128)S(1)}, u32[]{:S(2)}, u32[]{:S(2)}) collective-permute-start(f32[3,2,128]{2,1,0:T(2,128)S(1)} %get-tuple-element.15), channel_id=1, source_target_pairs={{0,1},{1,2},{2,3},{3,4},{4,5},{5,6},{6,7},{7,8},{8,9},{9,10},{10,1... | collective-permute-start | bytes 9224 | tf_op jit(solution)/shard_map/ppermute | solution.py:142
  5.7 1.9 %collective-permute-start.1 = (f32[3,2,128]{2,1,0:T(2,128)S(1)}, f32[3,2,128]{2,1,0:T(2,128)S(1)}, u32[]{:S(2)}, u32[]{:S(2)}) collective-permute-start(f32[3,2,128]{2,1,0:T(2,128)S(1)} %get-tuple-element.16), channel_id=1, source_target_pairs={{1,0},{2,1},{3,2},{4,3},{5,4},{6,5},{7,6},{8,7},{9,8},{10,9},{11,1... | collective-permute-start | bytes 9224 | tf_op jit(solution)/shard_map/ppermute | solution.py:143
  7.6 0.8 copy.40
  8.4 0.7 copy.37
  9.1 0.7 iota_compare_fusion.1
  9.8 0.9 broadcast_subtract_fusion
  10.8 1.1 copy.39
  11.8 0.1 reshape.80
  11.9 0.1 copy.41
  12.0 0.0 copy-done.1
  12.0 0.1 pad_add_fusion
  12.1 36.3 %all_gather.10 = s32[28,1024]{0,1:T(8,128)S(1)} all-gather(s32[28,32]{0,1:T(8,128)S(1)} %pad_add_fusion), channel_id=1, replica_groups=mesh['dom'=32] {'dom'}, dimensions={1}, use_global_device_ids=true | all-gather | bytes 118272 | tf_op jit(solution)/shard_map/all_gather | solution.py:131
  48.4 0.4 slice_reduce_fusion
  48.8 0.1 pad_maximum_fusion
  48.9 43.3 %all_gather.11 = f32[246,1024]{0,1:T(8,128)S(1)} all-gather(f32[246,32]{0,1:T(8,128)S(1)} %pad_maximum_fusion), channel_id=1, replica_groups=mesh['dom'=32] {'dom'}, dimensions={1}, use_global_device_ids=true | all-gather | bytes 1039104 | tf_op jit(solution)/shard_map/all_gather | solution.py:130
  92.2 0.7 slice_subtract_fusion.index_ref
  92.9 1.1 select_reduce_fusion
  94.0 1.4 reshape.76
  95.4 0.0 copy-start.2
  95.4 1.0 copy.34.block_ref
  96.4 0.0 collective-permute-done
  96.4 0.0 collective-permute-done.1
  96.4 0.6 pad_maximum_fusion.1.pad_ref
  97.1 2.5 %shard_map.104.field_ref = f32[3,8,128]{2,1,0:T(8,128)} custom-call(f32[3,12,128]{2,1,0:T(8,128)} %pad_maximum_fusion.1.pad_ref, s32[27,8,128]{2,1,0:T(8,128)} %slice_subtract_fusion.index_ref, f32[27,3,3,8,128]{4,3,2,1,0:T(8,128)} %copy.34.block_ref, f32[3,8,128]{2,1,0:T(8,128)} %get-tuple-element.8.diagonal_ref, f32[3,8,128]{2,1,0:T(8,128)} %get-tuple-element.7.right_ref), custom_call_target="tpu_custom_call" | custom-call | tf_op jit(solution)/shard_map/pallas_call | solution.py:145
  99.6 0.8 fusion.2
  100.3 1.9 %collective-permute-start.2 = (f32[3,2,128]{2,1,0:T(2,128)S(1)}, f32[3,2,128]{2,1,0:T(2,128)S(1)}, u32[]{:S(2)}, u32[]{:S(2)}) collective-permute-start(f32[3,2,128]{2,1,0:T(2,128)S(1)} %get-tuple-element.13), channel_id=1, source_target_pairs={{0,1},{1,2},{2,3},{3,4},{4,5},{5,6},{6,7},{7,8},{8,9},{9,10},{10,1... | collective-permute-start | bytes 9224 | tf_op jit(solution)/shard_map/ppermute | solution.py:142
  102.3 2.4 %collective-permute-start.3 = (f32[3,2,128]{2,1,0:T(2,128)S(1)}, f32[3,2,128]{2,1,0:T(2,128)S(1)}, u32[]{:S(2)}, u32[]{:S(2)}) collective-permute-start(f32[3,2,128]{2,1,0:T(2,128)S(1)} %get-tuple-element.14), channel_id=1, source_target_pairs={{1,0},{2,1},{3,2},{4,3},{5,4},{6,5},{7,6},{8,7},{9,8},{10,9},{11,1... | collective-permute-start | bytes 9224 | tf_op jit(solution)/shard_map/ppermute | solution.py:143
  104.7 0.5 pad_bitcast_fusion.own_ref
  105.2 0.8 copy.46.column_ref
  106.0 0.2 slice.55
  106.2 0.8 copy.47.diagonal_ref
  107.0 0.3 copy.42
  107.4 0.2 copy.53
  107.6 0.0 copy-start
  107.6 1.1 slice.59
  108.6 0.0 collective-permute-done.2
  108.6 0.3 collective-permute-done.3
  109.0 0.6 pad_maximum_fusion.2.pad_ref
  109.6 2.5 %shard_map.105 = f32[3,8,128]{2,1,0:T(8,128)} custom-call(f32[3,12,128]{2,1,0:T(8,128)} %pad_maximum_fusion.2.pad_ref, s32[27,8,128]{2,1,0:T(8,128)} %slice_subtract_fusion.index_ref, f32[27,3,3,8,128]{4,3,2,1,0:T(8,128)} %copy.34.block_ref, f32[3,8,128]{2,1,0:T(8,128)} %get-tuple-element.8.diagonal_ref, f32[3,8,128]{2,1,0:T(8,128)} %get-tuple-element.7.right_ref), custom_call_target="tpu_custom_call" | custom-call | tf_op jit(solution)/shard_map/pallas_call | solution.py:145
  112.1 0.7 copy.66
  112.8 0.1 select_reduce_fusion.1
  112.9 35.7 %all-gather = f32[32,32,3]{1,2,0:T(4,128)S(1)} all-gather(f32[1,32,3]{1,2,0:T(4,128)S(1)} %bitcast.83), channel_id=1, replica_groups=mesh['dom'=32] {'dom'}, dimensions={0}, use_global_device_ids=true | all-gather | bytes 12672 | tf_op jit(solution)/shard_map/all_gather | solution.py:157
  148.6 0.1 reshape.88
  148.7 0.6 copy.67
  149.3 7.1 %shard_map.106 = (f32[3,8,128]{2,1,0:T(8,128)}, f32[3,8,128]{2,1,0:T(8,128)}) custom-call(f32[3,8,128]{2,1,0:T(8,128)} %bitcast.73, s32[8,128]{1,0:T(8,128)} %bitcast.84, s32[27,8,128]{2,1,0:T(8,128)} %copy.46.column_ref, f32[27,3,3,8,128]{4,3,2,1,0:T(8,128)} %bitcast.64, f32[3,8,128]{2,1,0:T(8,128)} %copy.47.diagonal_ref, s32[8,128]{1,0:T(8,128)} %bitcast.77, ...), custom_call_target="tpu_custom_call" | custom-call | tf_op jit(solution)/shard_map/pallas_call | solution.py:158
  156.4 0.8 fusion.1
  157.2 3.6 %collective-permute-start.4 = (f32[3,2,128]{2,1,0:T(2,128)S(1)}, f32[3,2,128]{2,1,0:T(2,128)S(1)}, u32[]{:S(2)}, u32[]{:S(2)}) collective-permute-start(f32[3,2,128]{2,1,0:T(2,128)S(1)} %get-tuple-element.11), channel_id=1, source_target_pairs={{0,1},{1,2},{2,3},{3,4},{4,5},{5,6},{6,7},{7,8},{8,9},{9,10},{10,1... | collective-permute-start | bytes 9224 | tf_op jit(solution)/shard_map/ppermute | solution.py:142
  160.8 1.9 %collective-permute-start.5 = (f32[3,2,128]{2,1,0:T(2,128)S(1)}, f32[3,2,128]{2,1,0:T(2,128)S(1)}, u32[]{:S(2)}, u32[]{:S(2)}) collective-permute-start(f32[3,2,128]{2,1,0:T(2,128)S(1)} %get-tuple-element.12), channel_id=1, source_target_pairs={{1,0},{2,1},{3,2},{4,3},{5,4},{6,5},{7,6},{8,7},{9,8},{10,9},{11,1... | collective-permute-start | bytes 9224 | tf_op jit(solution)/shard_map/ppermute | solution.py:143
  162.7 0.7 copy.64
  163.4 0.0 collective-permute-done.4
  163.4 4.1 %collective-permute-done.5 = f32[3,2,128]{2,1,0:T(2,128)S(1)} collective-permute-done((f32[3,2,128]{2,1,0:T(2,128)S(1)}, f32[3,2,128]{2,1,0:T(2,128)S(1)}, u32[]{:S(2)}, u32[]{:S(2)}) %collective-permute-start.5) | collective-permute-done | bytes 3104 | tf_op jit(solution)/shard_map/ppermute | solution.py:143
  167.5 1.3 pad_maximum_fusion.3.pad_ref
  168.8 2.5 %shard_map.107 = f32[3,8,128]{2,1,0:T(8,128)} custom-call(f32[3,12,128]{2,1,0:T(8,128)} %pad_maximum_fusion.3.pad_ref, s32[27,8,128]{2,1,0:T(8,128)} %slice_subtract_fusion.index_ref, f32[27,3,3,8,128]{4,3,2,1,0:T(8,128)} %copy.34.block_ref, f32[3,8,128]{2,1,0:T(8,128)} %get-tuple-element.8.diagonal_ref, f32[3,8,128]{2,1,0:T(8,128)} %get-tuple-element.7.right_ref), custom_call_target="tpu_custom_call" | custom-call | tf_op jit(solution)/shard_map/pallas_call | solution.py:145
  171.3 0.8 fusion
  172.1 1.9 %collective-permute-start.6 = (f32[3,2,128]{2,1,0:T(2,128)S(1)}, f32[3,2,128]{2,1,0:T(2,128)S(1)}, u32[]{:S(2)}, u32[]{:S(2)}) collective-permute-start(f32[3,2,128]{2,1,0:T(2,128)S(1)} %get-tuple-element.9), channel_id=1, source_target_pairs={{0,1},{1,2},{2,3},{3,4},{4,5},{5,6},{6,7},{7,8},{8,9},{9,10},{10,1... | collective-permute-start | bytes 9224 | tf_op jit(solution)/shard_map/ppermute | solution.py:142
  174.0 2.4 %collective-permute-start.7 = (f32[3,2,128]{2,1,0:T(2,128)S(1)}, f32[3,2,128]{2,1,0:T(2,128)S(1)}, u32[]{:S(2)}, u32[]{:S(2)}) collective-permute-start(f32[3,2,128]{2,1,0:T(2,128)S(1)} %get-tuple-element.10), channel_id=1, source_target_pairs={{1,0},{2,1},{3,2},{4,3},{5,4},{6,5},{7,6},{8,7},{9,8},{10,9},{11,1... | collective-permute-start | bytes 9224 | tf_op jit(solution)/shard_map/ppermute | solution.py:143
  176.4 0.7 dynamic-slice_bitcast_fusion
  177.1 0.0 collective-permute-done.6
  177.1 3.7 %collective-permute-done.7 = f32[3,2,128]{2,1,0:T(2,128)S(1)} collective-permute-done((f32[3,2,128]{2,1,0:T(2,128)S(1)}, f32[3,2,128]{2,1,0:T(2,128)S(1)}, u32[]{:S(2)}, u32[]{:S(2)}) %collective-permute-start.7) | collective-permute-done | bytes 3104 | tf_op jit(solution)/shard_map/ppermute | solution.py:143
  180.8 1.3 pad_maximum_fusion.4.pad_ref
  182.1 2.5 %shard_map.108 = f32[3,8,128]{2,1,0:T(8,128)} custom-call(f32[3,12,128]{2,1,0:T(8,128)} %pad_maximum_fusion.4.pad_ref, s32[27,8,128]{2,1,0:T(8,128)} %slice_subtract_fusion.index_ref, f32[27,3,3,8,128]{4,3,2,1,0:T(8,128)} %copy.34.block_ref, f32[3,8,128]{2,1,0:T(8,128)} %get-tuple-element.8.diagonal_ref, f32[3,8,128]{2,1,0:T(8,128)} %get-tuple-element.7.right_ref), custom_call_target="tpu_custom_call" | custom-call | tf_op jit(solution)/shard_map/pallas_call | solution.py:145
  184.6 1.3 copy.65
  (6 shorter events, 0.0 us)
Async XLA Ops:
  0.6 11.3 %copy-start.1 = (s32[32,27]{1,0:T(8,128)S(1)}, s32[32,27]{1,0:T(8,128)}, u32[]{:S(2)}) copy-start(s32[32,27]{1,0:T(8,128)} %param.16) | copy-start | bytes 10372
  2.0 94.5 %collective-permute-start = (f32[3,2,128]{2,1,0:T(2,128)S(1)}, f32[3,2,128]{2,1,0:T(2,128)S(1)}, u32[]{:S(2)}, u32[]{:S(2)}) collective-permute-start(f32[3,2,128]{2,1,0:T(2,128)S(1)} %get-tuple-element.15), channel_id=1, source_target_pairs={{0,1},{1,2},{2,3},{3,4},{4,5},{5,6},{6,7},{7,8},{8,9},{9,10},{10,1... | collective-permute-start | bytes 9224 | tf_op jit(solution)/shard_map/ppermute | solution.py:142
  5.7 90.8 %collective-permute-start.1 = (f32[3,2,128]{2,1,0:T(2,128)S(1)}, f32[3,2,128]{2,1,0:T(2,128)S(1)}, u32[]{:S(2)}, u32[]{:S(2)}) collective-permute-start(f32[3,2,128]{2,1,0:T(2,128)S(1)} %get-tuple-element.16), channel_id=1, source_target_pairs={{1,0},{2,1},{3,2},{4,3},{5,4},{6,5},{7,6},{8,7},{9,8},{10,9},{11,1... | collective-permute-start | bytes 9224 | tf_op jit(solution)/shard_map/ppermute | solution.py:143
  95.4 9.3 %copy-start.2 = (s32[32]{0:T(128)S(1)}, s32[32]{0:T(128)}, u32[]{:S(2)}) copy-start(s32[32]{0:T(128)} %param.14) | copy-start | bytes 388
  100.3 8.3 %collective-permute-start.2 = (f32[3,2,128]{2,1,0:T(2,128)S(1)}, f32[3,2,128]{2,1,0:T(2,128)S(1)}, u32[]{:S(2)}, u32[]{:S(2)}) collective-permute-start(f32[3,2,128]{2,1,0:T(2,128)S(1)} %get-tuple-element.13), channel_id=1, source_target_pairs={{0,1},{1,2},{2,3},{3,4},{4,5},{5,6},{6,7},{7,8},{8,9},{9,10},{10,1... | collective-permute-start | bytes 9224 | tf_op jit(solution)/shard_map/ppermute | solution.py:142
  102.3 6.7 %collective-permute-start.3 = (f32[3,2,128]{2,1,0:T(2,128)S(1)}, f32[3,2,128]{2,1,0:T(2,128)S(1)}, u32[]{:S(2)}, u32[]{:S(2)}) collective-permute-start(f32[3,2,128]{2,1,0:T(2,128)S(1)} %get-tuple-element.14), channel_id=1, source_target_pairs={{1,0},{2,1},{3,2},{4,3},{5,4},{6,5},{7,6},{8,7},{9,8},{10,9},{11,1... | collective-permute-start | bytes 9224 | tf_op jit(solution)/shard_map/ppermute | solution.py:143
  107.6 1.4 copy-start
  157.2 6.2 %collective-permute-start.4 = (f32[3,2,128]{2,1,0:T(2,128)S(1)}, f32[3,2,128]{2,1,0:T(2,128)S(1)}, u32[]{:S(2)}, u32[]{:S(2)}) collective-permute-start(f32[3,2,128]{2,1,0:T(2,128)S(1)} %get-tuple-element.11), channel_id=1, source_target_pairs={{0,1},{1,2},{2,3},{3,4},{4,5},{5,6},{6,7},{7,8},{8,9},{9,10},{10,1... | collective-permute-start | bytes 9224 | tf_op jit(solution)/shard_map/ppermute | solution.py:142
  160.8 6.7 %collective-permute-start.5 = (f32[3,2,128]{2,1,0:T(2,128)S(1)}, f32[3,2,128]{2,1,0:T(2,128)S(1)}, u32[]{:S(2)}, u32[]{:S(2)}) collective-permute-start(f32[3,2,128]{2,1,0:T(2,128)S(1)} %get-tuple-element.12), channel_id=1, source_target_pairs={{1,0},{2,1},{3,2},{4,3},{5,4},{6,5},{7,6},{8,7},{9,8},{10,9},{11,1... | collective-permute-start | bytes 9224 | tf_op jit(solution)/shard_map/ppermute | solution.py:143
  172.1 5.0 %collective-permute-start.6 = (f32[3,2,128]{2,1,0:T(2,128)S(1)}, f32[3,2,128]{2,1,0:T(2,128)S(1)}, u32[]{:S(2)}, u32[]{:S(2)}) collective-permute-start(f32[3,2,128]{2,1,0:T(2,128)S(1)} %get-tuple-element.9), channel_id=1, source_target_pairs={{0,1},{1,2},{2,3},{3,4},{4,5},{5,6},{6,7},{7,8},{8,9},{9,10},{10,1... | collective-permute-start | bytes 9224 | tf_op jit(solution)/shard_map/ppermute | solution.py:142
  174.0 6.7 %collective-permute-start.7 = (f32[3,2,128]{2,1,0:T(2,128)S(1)}, f32[3,2,128]{2,1,0:T(2,128)S(1)}, u32[]{:S(2)}, u32[]{:S(2)}) collective-permute-start(f32[3,2,128]{2,1,0:T(2,128)S(1)} %get-tuple-element.10), channel_id=1, source_target_pairs={{1,0},{2,1},{3,2},{4,3},{5,4},{6,5},{7,6},{8,7},{9,8},{10,9},{11,1... | collective-permute-start | bytes 9224 | tf_op jit(solution)/shard_map/ppermute | solution.py:143
